TPU v7x, 32 devices: a whole 2x2x4 slice. The times are simulated.
32 devices in a mesh: vocab: 32 (over z, y, x, core).
Axes of the slice: x: 2, y: 2, z: 4, core: 2. Of those that a mesh axis runs over, the one named last changes fastest.
Arguments:
- hidden: bfloat16 [2, 256, 3584], P(None, 'vocab'), may hold values from -256 to 256
- head_weight: bfloat16 [3584, 24576], P(None, 'vocab'), may hold values from -1 to 1
- teacher: bfloat16 [2, 256, 24576], P(None, None, 'vocab'), may hold values from 0 to 1
Outputs:
- token_loss: float32 [2, 256], P(None, 'vocab')
- hidden_grad: bfloat16 [2, 256, 3584], P(None, 'vocab')
- head_grad: bfloat16 [3584, 24576], P(None, 'vocab')
All inputs are finite; a program needn't handle non-finite values.
Results may differ from a plain program's by a relative error of at most 0.012.
Values may be sent and summed in bfloat16 or wider, within the bound.
No kernel may reach another device: no remote copies, remote signals or barrier semaphores. Data moves between devices by JAX's collectives and lax.ppermute only.
A program may use at most 128 MiB of HBM per device.

v0:
```python
import jax
import jax.numpy as jnp
from jax import lax
from jax.sharding import PartitionSpec as P


def finish(logit_block, target_block):
    target_wide = target_block.astype(jnp.float32)
    teacher_mass = jnp.sum(target_wide, axis=-1)
    cross_term = jnp.sum(target_wide * logit_block, axis=-1)
    peak_logit = jnp.max(logit_block, axis=-1)
    peak_logit = lax.pmax(peak_logit, "vocab")
    exp_total = jnp.sum(jnp.exp(logit_block - peak_logit[..., None]), axis=-1)
    exp_total, teacher_mass, cross_term = lax.psum((exp_total, teacher_mass, cross_term), "vocab")
    log_norm = peak_logit + jnp.log(exp_total)
    token_loss = teacher_mass * log_norm - cross_term
    logit_grad = (
        teacher_mass[..., None] * jnp.exp(logit_block - log_norm[..., None]) - target_wide
    ).astype(jnp.bfloat16)
    return (token_loss, logit_grad)


def shards(hidden, head_weight, teacher):
    group_count, row_count, model_width = hidden.shape
    contract = (((1,), (1,)), ((), ()))
    shard_rows = lax.all_gather(hidden, "vocab", axis=1, tiled=True)
    logits = jnp.einsum("crd,dv->crv", shard_rows, head_weight, preferred_element_type=jnp.float32)
    token_loss, logit_grad = finish(logits, teacher)
    row_total = lax.axis_size("vocab") * (group_count * row_count)
    per_group = row_total // group_count
    owner_count = per_group // row_count
    grad_block = logit_grad
    grad_block = (
        grad_block.reshape(group_count, owner_count, row_count, -1)
        .transpose(1, 0, 2, 3)
        .reshape(row_total, -1)
    )
    summed = lax.psum_scatter(
        lax.dot_general(grad_block, head_weight, contract, preferred_element_type=jnp.float32),
        "vocab",
        scatter_dimension=0,
        tiled=True,
    )
    hidden_grad = summed.reshape(group_count, row_count, model_width).astype(jnp.bfloat16)
    weight_grad = jnp.zeros((model_width, head_weight.shape[1]), jnp.bfloat16)
    for group_index in range(group_count):
        product_term = lax.dot_general(
            shard_rows[group_index],
            logit_grad[group_index],
            (((0,), (0,)), ((), ())),
            preferred_element_type=jnp.float32,
        )
        weight_grad = (weight_grad.astype(jnp.float32) + product_term).astype(jnp.bfloat16)
    own_loss = lax.dynamic_slice_in_dim(
        token_loss, lax.axis_index("vocab") * row_count, row_count, 1
    )
    return (own_loss, hidden_grad, weight_grad)


def solution(mesh):
    in_specs = (P(None, "vocab", None), P(None, "vocab"), P(None, None, "vocab"))
    out_specs = (P(None, "vocab"), P(None, "vocab", None), P(None, "vocab"))
    return jax.shard_map(shards, mesh=mesh, in_specs=in_specs, out_specs=out_specs, check_vma=False)
```

profile of v0, /device:TPU:0, one launch (start us, length us, event | category | flops | bytes accessed | tf_op | source)
XLA Modules:
  0.0 325.6 jit_solution(7871215503381196824)
XLA Ops:
  7.2 0.0 all-gather.2.cloned.1.call-start
  7.2 0.7 all-gather.2.cloned.1.call-update
  7.9 0.0 copy-start.1
  7.9 0.0 reduce-scatter.2.cloned.1.call-start
  8.0 66.4 %all-gather.2.cloned.1.call-done = bf16[2,256,3584]{2,1,0:T(8,128)(2,1)} async-done(((bf16[2,8,3584]{2,1,0:T(8,128)(2,1)}), bf16[2,256,3584]{2,1,0:T(8,128)(2,1)}) %all-gather.2.cloned.1.call-update) | async-done | bytes 3670032 | tf_op jit(solution)/shard_map/all_gather | solution.py:26
  74.3 6.8 %fusion.5 = (f32[2,256]{1,0:T(2,128)S(1)}, f32[2,256,768]{2,1,0:T(8,128)S(1)}) fusion(bf16[2,256,3584]{2,1,0:T(8,128)(2,1)} %all-gather.2.cloned.1.call-done, bf16[3584,768]{1,0:T(8,128)(2,1)} %param.4), kind=kOutput, calls=%fused_computation.19 | convolution fusion | flops 2818964992 | bytes 10749952 | tf_op jit(solution)/shard_map/crd,dv->crv/dot_general | solution.py:27
  81.1 38.5 %pmax.7 = f32[2,256]{1,0:T(2,128)S(1)} all-reduce(f32[2,256]{1,0:T(2,128)S(1)} %get-tuple-element.15), channel_id=1, replica_groups=mesh['vocab'=32] {'vocab'}, use_global_device_ids=true, to_apply=%region_3.0 | all-reduce | flops 512 | bytes 4096 | tf_op jit(solution)/shard_map/pmax | solution.py:12
  119.6 0.0 copy-done.1
  119.6 0.7 exponential_reduce_fusion
  120.4 40.7 %all-reduce = (f32[2,256]{1,0:T(2,128)S(1)}, f32[2,256]{1,0:T(2,128)S(1)}, f32[2,256]{1,0:T(2,128)S(1)}) all-reduce(f32[2,256]{1,0:T(2,128)S(1)} %get-tuple-element.10, f32[2,256]{1,0:T(2,128)S(1)} %get-tuple-element.9, f32[2,256]{1,0:T(2,128)S(1)} %get-tuple-element.11), channel_id=1, replica_groups=mesh['vocab'=32] {'vocab'}, use_global_device_ids=true, to_apply=%region_7.0 | all-reduce | flops 1536 | bytes 12288 | tf_op jit(solution)/shard_map/psum | solution.py:14
  161.0 0.4 fusion.4
  161.5 0.1 copy.7
  161.5 7.7 %fusion.6 = f32[512,3584]{1,0:T(8,128)} fusion(bf16[512,768]{1,0:T(8,128)(2,1)S(1)} %bitcast.29, bf16[3584,768]{1,0:T(8,128)(2,1)} %param.4), kind=kOutput, calls=%fused_computation.20 | convolution fusion | flops 2818572288 | bytes 13631488 | tf_op jit(solution)/shard_map/dot_general | solution.py:39
  169.2 0.0 reduce-scatter.2.cloned.1.call-update
  169.3 0.0 copy-start
  169.3 3.3 %convolution_convert_fusion = bf16[768,3584]{1,0:T(8,128)(2,1)S(1)} fusion(bf16[2,256,3584]{2,1,0:T(8,128)(2,1)} %all-gather.2.cloned.1.call-done, bf16[2,256,768]{2,1,0:T(8,128)(2,1)S(1)} %fusion.4), kind=kOutput, calls=%fused_computation.1 | convolution fusion | flops 1412038656 | bytes 7733248 | tf_op jit(solution)/shard_map/dot_general | solution.py:47
  172.6 0.0 copy-done
  172.6 4.0 %fusion = bf16[3584,768]{0,1:T(8,128)(2,1)} fusion(bf16[768,3584]{1,0:T(8,128)(2,1)S(1)} %convolution_convert_fusion, bf16[2,256,3584]{2,1,0:T(8,128)(2,1)S(1)} %copy-done, bf16[2,256,768]{2,1,0:T(8,128)(2,1)S(1)} %fusion.4), kind=kOutput, calls=%fused_computation.2 | convolution fusion | flops 1417543680 | bytes 13238272 | tf_op jit(solution)/shard_map/dot_general | solution.py:47
  176.6 8.3 %copy.8 = bf16[3584,768]{1,0:T(8,128)(2,1)} copy(bf16[3584,768]{0,1:T(8,128)(2,1)} %fusion) | data formatting | bytes 11010048
  184.9 0.6 dynamic-slice_subtract_fusion
  185.5 131.7 %reduce-scatter.2.cloned.1.call-done = f32[16,3584]{1,0:T(8,128)} async-done(((f32[512,3584]{1,0:T(8,128)}), f32[16,3584]{1,0:T(8,128)}) %reduce-scatter.2.cloned.1.call-update) | async-done | bytes 229392 | tf_op jit(solution)/shard_map/reduce_scatter | solution.py:38
  317.2 1.6 convert_bitcast_fusion
  (1 shorter events, 0.0 us)
Async XLA Ops:
  7.2 67.2 %all-gather.2.cloned.1.call-start = ((), (), s32[]{:S(2)}) async-start(), calls=%async_computation.1 | async-start | bytes 3784704 | tf_op jit(solution)/shard_map/all_gather | solution.py:26
  7.9 111.7 %copy-start.1 = (bf16[2,256,768]{2,1,0:T(8,128)(2,1)S(1)}, bf16[2,256,768]{2,1,0:T(8,128)(2,1)}, u32[]{:S(2)}) copy-start(bf16[2,256,768]{2,1,0:T(8,128)(2,1)} %param.5) | copy-start | bytes 2359300
  7.9 309.3 %reduce-scatter.2.cloned.1.call-start = ((), (), s32[]{:S(2)}) async-start(), calls=%async_computation.2 | async-start | bytes 7569408 | tf_op jit(solution)/shard_map/reduce_scatter | solution.py:38
  169.3 3.3 %copy-start = (bf16[2,256,3584]{2,1,0:T(8,128)(2,1)S(1)}, bf16[2,256,3584]{2,1,0:T(8,128)(2,1)}, u32[]{:S(2)}) copy-start(bf16[2,256,3584]{2,1,0:T(8,128)(2,1)} %all-gather.2.cloned.1.call-done) | copy-start | bytes 11010052
Sparse Core Ops, SparseCore 0:
  10.9 63.4 all-gather.1
  169.4 147.7 reduce-scatter.1
where the time goes:
time: 326 us
  waiting for transfers between devices  199 us (61%)
  blocking collectives  79.2 us (24%)
  matrix products  21.8 us (7%)
  between operations  14.1 us (4%)
  local copies, waits for them, and re-layouts  8.33 us (3%)
  other arithmetic  3.38 us (1%)
    reduce_scatter x1, waiting for transfers between devices, shards(): lax.psum_scatter(lax.dot_general(grad_block, head_weight, contract, prefe...  132 us
    all_gather x1, waiting for transfers between devices, shards(): shard_rows = lax.all_gather(hidden, 'vocab', axis=1, tiled=True)  66.4 us
    psum x1, blocking collectives, finish(): lax.psum((exp_total, teacher_mass, cross_term), 'vocab')  40.7 us
    pmax x1, blocking collectives, finish(): peak_logit = lax.pmax(peak_logit, 'vocab')  38.5 us
    unnamed x5, local copies, waits for them, and re-layouts  8.28 us
    dot_general x1, matrix products, shards(): lax.dot_general(grad_block, head_weight, contract, preferred_element_type...  7.71 us
    dot_general x2, matrix products, shards(): lax.dot_general(shard_rows[group_index], logit_grad[group_index], (((0,),...  7.29 us
    dot_general x1, matrix products, shards(): jnp.einsum('crd,dv->crv', shard_rows, head_weight, preferred_element_type...  6.76 us
  transfers between devices with their start and end apart: 2, of which 2 were waited for; matrix products, arithmetic and copies ran while one was open for 5% of the time, Pallas kernels for 0%

commit v1 on v0

v1 whole, which is shorter than its diff:
```python
import functools

import jax
import jax.numpy as jnp
from jax import lax
from jax.experimental import pallas as pl
from jax.experimental.pallas import tpu as pltpu
from jax.sharding import PartitionSpec as P

AXIS = "vocab"
ROW_TILE = 8


def stage_orders(size):
    bits = list(range(size.bit_length() - 2, 0, -1))
    low, high = [], []
    for start in range(0, len(bits), 2):
        pair = bits[start : start + 2]
        low += pair[::-1]
        high += pair
    return low, high


def masks_of(order):
    masks = [0]
    for bit in order:
        masks += [mask | (1 << bit) for mask in masks]
    return masks


def owner_of(me, masks, block):
    half = len(masks[0])
    core = lax.rem(me, 2)
    if block < half:
        return me ^ jnp.where(core == 0, masks[0][block], masks[1][block])
    block -= half
    return me ^ 1 ^ jnp.where(core == 0, masks[1][block], masks[0][block])


def swap(value, order_pair, stage, size):
    pairs = [(i, i ^ (1 << order_pair[i & 1][stage])) for i in range(size)]
    return lax.ppermute(value, AXIS, pairs)


def swap_core(value, size):
    return lax.ppermute(value, AXIS, [(i, i ^ 1) for i in range(size)])


def stats_kernel(masks, me_ref, own_ref, pair_ref, teacher_ref, out_ref):
    me = me_ref[0]
    groups = own_ref.shape[0]
    half = len(masks[0])
    size = 2 * half
    lane = lax.broadcasted_iota(jnp.int32, (ROW_TILE, groups * size), 1)
    norm_all = jnp.zeros((ROW_TILE, groups * size), jnp.float32)
    mass_all = norm_all
    cross_all = norm_all
    for block in range(size):
        owner = owner_of(me, masks, block)
        start = pl.multiple_of(owner * ROW_TILE, ROW_TILE)
        source = own_ref if block < half else pair_ref
        rows = pl.ds((block % half) * ROW_TILE, ROW_TILE)
        for group in range(groups):
            logits = source[group, rows, :]
            target = teacher_ref[group, pl.ds(start, ROW_TILE), :].astype(jnp.float32)
            peak = jnp.max(logits, axis=1, keepdims=True)
            total = jnp.sum(jnp.exp(logits - peak), axis=1, keepdims=True)
            mass = jnp.sum(target, axis=1, keepdims=True)
            cross = jnp.sum(target * logits, axis=1, keepdims=True)
            here = lane == group * size + owner
            norm_all = jnp.where(here, peak + jnp.log(total), norm_all)
            mass_all = jnp.where(here, mass, mass_all)
            cross_all = jnp.where(here, cross, cross_all)
    out_ref[0] = norm_all
    out_ref[1] = mass_all
    out_ref[2] = cross_all


def grad_kernel(masks, me_ref, stats_ref, own_ref, pair_ref, teacher_ref, loss_ref, own_grad_ref, pair_grad_ref):
    me = me_ref[0]
    groups = own_ref.shape[0]
    half = len(masks[0])
    size = 2 * half
    norms = stats_ref[:, 0]
    peak = jnp.max(norms, axis=0)
    log_norm = peak + jnp.log(jnp.sum(jnp.exp(norms - peak[None]), axis=0))
    mass = jnp.sum(stats_ref[:, 1], axis=0)
    cross = jnp.sum(stats_ref[:, 2], axis=0)
    loss_ref[...] = mass * log_norm - cross
    lane = lax.broadcasted_iota(jnp.int32, mass.shape, 1)
    for block in range(size):
        owner = owner_of(me, masks, block)
        start = pl.multiple_of(owner * ROW_TILE, ROW_TILE)
        source = own_ref if block < half else pair_ref
        result = own_grad_ref if block < half else pair_grad_ref
        rows = pl.ds((block % half) * ROW_TILE, ROW_TILE)
        for group in range(groups):
            here = lane == group * size + owner
            norm_rows = jnp.sum(jnp.where(here, log_norm, 0.0), axis=1, keepdims=True)
            mass_rows = jnp.sum(jnp.where(here, mass, 0.0), axis=1, keepdims=True)
            target = teacher_ref[group, pl.ds(start, ROW_TILE), :].astype(jnp.float32)
            grad = mass_rows * jnp.exp(source[group, rows, :] - norm_rows) - target
            result[group, rows, :] = grad.astype(jnp.bfloat16)


def vmem(count):
    return [pl.BlockSpec(memory_space=pltpu.VMEM)] * count


def call_stats(me, own, pair, teacher, masks):
    size = 2 * len(masks[0])
    return pl.pallas_call(
        functools.partial(stats_kernel, masks),
        out_shape=jax.ShapeDtypeStruct((3, ROW_TILE, own.shape[0] * size), jnp.float32),
        in_specs=[pl.BlockSpec(memory_space=pltpu.SMEM)] + vmem(3),
        out_specs=vmem(1)[0],
        cost_estimate=pl.CostEstimate(flops=2_000_000, bytes_accessed=2_400_000, transcendentals=400_000),
        name="stats",
    )(me, own, pair, teacher)


def call_grad(me, stats, own, pair, teacher, masks):
    grad = jax.ShapeDtypeStruct(own.shape, jnp.bfloat16)
    return pl.pallas_call(
        functools.partial(grad_kernel, masks),
        out_shape=(jax.ShapeDtypeStruct(stats.shape[2:], jnp.float32), grad, grad),
        in_specs=[pl.BlockSpec(memory_space=pltpu.SMEM)] + vmem(4),
        out_specs=tuple(vmem(3)),
        cost_estimate=pl.CostEstimate(flops=2_000_000, bytes_accessed=3_200_000, transcendentals=400_000),
        name="grad",
    )(me, stats, own, pair, teacher)


def plain_stats(owners, own, pair, teacher):
    groups, _, row_count, width = teacher.shape
    logits = jnp.concatenate([own, pair], axis=1).reshape(groups, -1, row_count, width)
    target = jnp.take(teacher, owners, axis=1).astype(jnp.float32)
    peak = jnp.max(logits, axis=-1)
    norm = peak + jnp.log(jnp.sum(jnp.exp(logits - peak[..., None]), axis=-1))
    stats = jnp.stack([norm, jnp.sum(target, axis=-1), jnp.sum(target * logits, axis=-1)])
    return jnp.zeros_like(stats).at[:, :, owners].set(stats)


def plain_grad(owners, stats, own, pair, teacher):
    groups, size, row_count, width = teacher.shape
    logits = jnp.concatenate([own, pair], axis=1).reshape(groups, size, row_count, width)
    norms = stats[:, 0]
    log_norm = jax.nn.logsumexp(norms, axis=0)
    mass = jnp.sum(stats[:, 1], axis=0)
    loss = mass * log_norm - jnp.sum(stats[:, 2], axis=0)
    target = jnp.take(teacher, owners, axis=1).astype(jnp.float32)
    scale = jnp.take(mass, owners, axis=1)[..., None]
    grad = scale * jnp.exp(logits - jnp.take(log_norm, owners, axis=1)[..., None]) - target
    grad = grad.astype(jnp.bfloat16).reshape(groups, size * row_count, width)
    return loss, grad[:, : size * row_count // 2], grad[:, size * row_count // 2 :]


def exchange_stats(stats, size):
    spread = jnp.broadcast_to(stats[None], (size, *stats.shape))
    return lax.all_to_all(spread, AXIS, 0, 0, tiled=True)


def matmul(left, right, contract):
    return lax.dot_general(left, right, (contract, ((), ())), preferred_element_type=jnp.float32)


def shards(hidden, head_weight, teacher):
    groups, row_count, model_width = hidden.shape
    size = lax.axis_size(AXIS)
    me = lax.axis_index(AXIS)
    orders = stage_orders(size)
    masks = tuple(masks_of(order) for order in orders)
    tiled = row_count == ROW_TILE
    stages = len(orders[0])

    held = hidden
    for stage in range(stages):
        held = jnp.concatenate([held, swap(held, orders, stage, size)], axis=1)
    other = swap_core(held, size)

    half_rows = held.shape[1]
    width = head_weight.shape[1]

    def project(rows):
        flat = matmul(rows.reshape(-1, model_width), head_weight, ((1,), (0,)))
        return flat.reshape(groups, half_rows, width)

    own_logits = project(held)
    pair_logits = project(other)
    if tiled:
        me_ref = me.reshape(1)
        stats = exchange_stats(call_stats(me_ref, own_logits, pair_logits, teacher, masks), size)
        loss, own_grad, pair_grad = call_grad(me_ref, stats, own_logits, pair_logits, teacher, masks)
        own_loss = lax.dynamic_index_in_dim(
            loss.reshape(row_count, groups, size), me, axis=2, keepdims=False
        ).T
    else:
        owners = jnp.stack([owner_of(me, masks, block) for block in range(size)])
        blocks = teacher.reshape(groups, size, row_count, width)
        stats = exchange_stats(plain_stats(owners, own_logits, pair_logits, blocks), size)
        loss, own_grad, pair_grad = plain_grad(owners, stats, own_logits, pair_logits, blocks)
        own_loss = lax.dynamic_index_in_dim(loss, me, axis=1, keepdims=False)

    def pull_back(grad):
        flat = matmul(grad.reshape(-1, width), head_weight, ((1,), (1,)))
        return flat.reshape(groups, half_rows, model_width)

    sent = swap_core(pull_back(pair_grad).astype(jnp.bfloat16), size)
    total = (pull_back(own_grad) + sent.astype(jnp.float32)).astype(jnp.bfloat16)
    for stage in reversed(range(stages)):
        rows = total.shape[1] // 2
        got = swap(total[:, rows:], orders, stage, size)
        total = (total[:, :rows].astype(jnp.float32) + got.astype(jnp.float32)).astype(jnp.bfloat16)

    flat = lambda value: value.reshape(-1, value.shape[-1])
    weight_grad = matmul(flat(held), flat(own_grad), ((0,), (0,)))
    weight_grad = weight_grad + matmul(flat(other), flat(pair_grad), ((0,), (0,)))
    return (own_loss, total, weight_grad.astype(jnp.bfloat16))


def solution(mesh):
    in_specs = (P(None, AXIS, None), P(None, AXIS), P(None, None, AXIS))
    out_specs = (P(None, AXIS), P(None, AXIS, None), P(None, AXIS))
    return jax.shard_map(shards, mesh=mesh, in_specs=in_specs, out_specs=out_specs, check_vma=False)
```

time: 326 us -> 130 us (0.40)
  waiting for transfers between devices: 199 us -> 60.7 us
  blocking collectives: 79.2 us -> 17.1 us
  between operations: 14.1 us -> 0.83 us
  starting transfers between devices: 0.08 us -> 12.1 us
  Pallas kernels: 0 us -> 5.93 us
  local copies, waits for them, and re-layouts: 8.33 us -> 4.35 us
    reduce_scatter x1 -> x0, waiting for transfers between devices: 132 us -> none  [shards(): lax.psum_scatter(lax.dot_general(grad_block, head_weight, contract, prefe...]
    all_gather x1 -> x0, waiting for transfers between devices: 66.4 us -> none  [shards(): shard_rows = lax.all_gather(hidden, 'vocab', axis=1, tiled=True)]
    ppermute x0 -> x10, waiting for transfers between devices: none -> 60.7 us  [the longest x8 57.3 us: swap(): return lax.ppermute(value, AXIS, pairs)]
    psum x1 -> x0, blocking collectives: 40.7 us -> none  [finish(): lax.psum((exp_total, teacher_mass, cross_term), 'vocab')]
    pmax x1 -> x0, blocking collectives: 38.5 us -> none  [finish(): peak_logit = lax.pmax(peak_logit, 'vocab')]
    all_to_all x0 -> x1, blocking collectives: none -> 17.1 us  [exchange_stats(): return lax.all_to_all(spread, AXIS, 0, 0, tiled=True)]
    ppermute x0 -> x10, starting transfers between devices: none -> 12.1 us  [the longest x8 11.5 us: swap(): return lax.ppermute(value, AXIS, pairs)]
    pallas_call x0 -> x2, Pallas kernels: none -> 5.93 us  [the longest x1 3.08 us: call_grad(): pl.pallas_call(functools.partial(grad_kernel, masks), out_shape=(jax.Shap...]
  transfers between devices with their start and end apart: 2 -> 10, of which waited for: 2 -> 8; matrix products, arithmetic and copies ran while one was open for 5% -> 11% of each run, Pallas kernels for 0% -> 0%
where the time goes in v1:
time: 130 us
  waiting for transfers between devices  60.7 us (47%)
  matrix products  22.5 us (17%)
  blocking collectives  17.1 us (13%)
  starting transfers between devices  12.1 us (9%)
  other arithmetic  5.97 us (5%)
  Pallas kernels  5.93 us (5%)
  local copies, waits for them, and re-layouts  4.35 us (3%)
    ppermute x8, waiting for transfers between devices, swap(): return lax.ppermute(value, AXIS, pairs)  57.3 us
    dot_general x6, matrix products, matmul(): lax.dot_general(left, right, (contract, ((), ())), preferred_element_type...  22.5 us
    all_to_all x1, blocking collectives, exchange_stats(): return lax.all_to_all(spread, AXIS, 0, 0, tiled=True)  17.1 us
    ppermute x8, starting transfers between devices, swap(): return lax.ppermute(value, AXIS, pairs)  11.5 us
    ppermute x2, waiting for transfers between devices, swap_core(): return lax.ppermute(value, AXIS, [(i, i ^ 1) for i in range(size)])  3.41 us
    pallas_call x1, Pallas kernels, call_grad(): pl.pallas_call(functools.partial(grad_kernel, masks), out_shape=(jax.Shap...  3.08 us
    pallas_call x1, Pallas kernels, call_stats(): pl.pallas_call(functools.partial(stats_kernel, masks), out_shape=jax.Shap...  2.85 us
    concatenate x3, other arithmetic, shards(): held = jnp.concatenate([held, swap(held, orders, stage, size)], axis=1)  2.8 us
  transfers between devices with their start and end apart: 10, of which 8 were waited for; matrix products, arithmetic and copies ran while one was open for 11% of the time, Pallas kernels for 0%

profile of v1, /device:TPU:0, one launch (start us, length us, event | category | flops | bytes accessed | tf_op | source)
XLA Modules:
  0.0 129.5 jit_solution(15900661249550817759)
XLA Ops:
  0.6 3.1 %collective-permute-start = (bf16[2,8,3584]{2,1,0:T(8,128)(2,1)}, bf16[2,8,3584]{2,1,0:T(8,128)(2,1)S(1)}, u32[]{:S(2)}, u32[]{:S(2)}) collective-permute-start(bf16[2,8,3584]{2,1,0:T(8,128)(2,1)} %param.3), channel_id=1, source_target_pairs={{0,8},{1,17},{2,10},{3,19},{4,12},{5,21},{6,14},{7,23},{8,0},{9,25... | collective-permute-start | bytes 344072 | tf_op jit(solution)/shard_map/ppermute | solution.py:42
  3.7 4.1 %collective-permute-done = bf16[2,8,3584]{2,1,0:T(8,128)(2,1)S(1)} collective-permute-done((bf16[2,8,3584]{2,1,0:T(8,128)(2,1)}, bf16[2,8,3584]{2,1,0:T(8,128)(2,1)S(1)}, u32[]{:S(2)}, u32[]{:S(2)}) %collective-permute-start) | collective-permute-done | bytes 114720 | tf_op jit(solution)/shard_map/ppermute | solution.py:42
  8.8 2.2 %collective-permute-start.1 = (bf16[2,16,3584]{2,1,0:T(8,128)(2,1)S(1)}, bf16[2,16,3584]{2,1,0:T(8,128)(2,1)S(1)}, u32[]{:S(2)}, u32[]{:S(2)}) collective-permute-start(bf16[2,16,3584]{2,1,0:T(8,128)(2,1)S(1)} %pad_maximum_fusion.2), channel_id=1, source_target_pairs={{0,16},{1,9},{2,18},{3,11},{4,20},{5,13},{6,22},{7,15},{8,24},{9,1... | collective-permute-start | bytes 688136 | tf_op jit(solution)/shard_map/ppermute | solution.py:42
  11.0 5.9 %collective-permute-done.1 = bf16[2,16,3584]{2,1,0:T(8,128)(2,1)S(1)} collective-permute-done((bf16[2,16,3584]{2,1,0:T(8,128)(2,1)S(1)}, bf16[2,16,3584]{2,1,0:T(8,128)(2,1)S(1)}, u32[]{:S(2)}, u32[]{:S(2)}) %collective-permute-start.1) | collective-permute-done | bytes 229408 | tf_op jit(solution)/shard_map/ppermute | solution.py:42
  17.8 1.9 %collective-permute-start.2 = (bf16[2,32,3584]{2,1,0:T(8,128)(2,1)S(1)}, bf16[2,32,3584]{2,1,0:T(8,128)(2,1)S(1)}, u32[]{:S(2)}, u32[]{:S(2)}) collective-permute-start(bf16[2,32,3584]{2,1,0:T(8,128)(2,1)S(1)} %pad_maximum_fusion.1), channel_id=1, source_target_pairs={{0,2},{1,5},{2,0},{3,7},{4,6},{5,1},{6,4},{7,3},{8,10},{9,13},{10,... | collective-permute-start | bytes 1376264 | tf_op jit(solution)/shard_map/ppermute | solution.py:42
  20.6 5.7 %collective-permute-done.2 = bf16[2,32,3584]{2,1,0:T(8,128)(2,1)S(1)} collective-permute-done((bf16[2,32,3584]{2,1,0:T(8,128)(2,1)S(1)}, bf16[2,32,3584]{2,1,0:T(8,128)(2,1)S(1)}, u32[]{:S(2)}, u32[]{:S(2)}) %collective-permute-start.2) | collective-permute-done | bytes 458784 | tf_op jit(solution)/shard_map/ppermute | solution.py:42
  26.3 1.0 pad_maximum_fusion
  27.3 1.9 %collective-permute-start.3 = (bf16[2,64,3584]{2,1,0:T(8,128)(2,1)S(1)}, bf16[2,64,3584]{2,1,0:T(8,128)(2,1)S(1)}, u32[]{:S(2)}, u32[]{:S(2)}) collective-permute-start(bf16[2,64,3584]{2,1,0:T(8,128)(2,1)S(1)} %pad_maximum_fusion), channel_id=1, source_target_pairs={{0,4},{1,3},{2,6},{3,1},{4,0},{5,7},{6,2},{7,5},{8,12},{9,11},{10,... | collective-permute-start | bytes 2752520 | tf_op jit(solution)/shard_map/ppermute | solution.py:42
  29.3 11.5 %collective-permute-done.3 = bf16[2,64,3584]{2,1,0:T(8,128)(2,1)S(1)} collective-permute-done((bf16[2,64,3584]{2,1,0:T(8,128)(2,1)S(1)}, bf16[2,64,3584]{2,1,0:T(8,128)(2,1)S(1)}, u32[]{:S(2)}, u32[]{:S(2)}) %collective-permute-start.3) | collective-permute-done | bytes 917536 | tf_op jit(solution)/shard_map/ppermute | solution.py:42
  40.9 5.2 %fusion.7.own_ref = f32[2,128,768]{2,1,0:T(8,128)} fusion(bf16[2,128,3584]{2,1,0:T(8,128)(2,1)S(1)} %constant_dynamic-update-slice_fusion, bf16[3584,768]{1,0:T(8,128)(2,1)} %param.4), kind=kOutput, calls=%fused_computation.8 | convolution fusion | flops 1409286144 | bytes 8126464 | tf_op jit(solution)/shard_map/dot_general | solution.py:164
  46.1 4.0 %fusion.5.pair_ref = f32[2,128,768]{2,1,0:T(8,128)} fusion(bf16[2,128,3584]{2,1,0:T(8,128)(2,1)} %collective-permute-done.4, bf16[3584,768]{1,0:T(8,128)(2,1)S(1)} %bitcast.33), kind=kOutput, calls=%fused_computation.6 | convolution fusion | flops 1409286144 | bytes 8126464 | tf_op jit(solution)/shard_map/dot_general | solution.py:164
  50.1 2.9 %stats.1 = f32[3,8,64]{2,1,0:T(8,128)} custom-call(s32[1]{0:T(128)} %bitcast.me_ref, f32[2,128,768]{2,1,0:T(8,128)} %fusion.7.own_ref, f32[2,128,768]{2,1,0:T(8,128)} %fusion.5.pair_ref, bf16[2,256,768]{2,1,0:T(8,128)(2,1)} %teacher_ref.3), custom_call_target="tpu_custom_call" | custom-call | flops 2000000 | bytes 2400000 | tf_op jit(solution)/shard_map/stats/pallas_call | solution.py:112
  53.9 17.1 %all_to_all.5 = f32[32,1,1536]{2,1,0:T(1,128)S(1)} all-to-all(f32[32,1,1536]{2,1,0:T(1,128)S(1)} %reshape.38), channel_id=1, replica_groups=mesh['vocab'=32] {'vocab'}, dimensions={0} | all-to-all | bytes 393216 | tf_op jit(solution)/shard_map/all_to_all | solution.py:160
  71.5 1.1 reduce
  73.5 3.1 %grad.1 = (f32[8,64]{1,0:T(8,128)}, bf16[2,128,768]{2,1,0:T(8,128)(2,1)}, bf16[2,128,768]{2,1,0:T(8,128)(2,1)}) custom-call(s32[1]{0:T(128)} %bitcast.me_ref, f32[32,3,8,64]{3,2,1,0:T(8,128)} %reshape.39.stats_ref, f32[2,128,768]{2,1,0:T(8,128)} %fusion.7.own_ref, f32[2,128,768]{2,1,0:T(8,128)} %fusion.5.pair_ref, bf16[2,256,768]{2,1,0:T(8,128)(2,1)} %teacher_ref.3), custom_call_target="tpu_custom_call" | custom-call | flops 2000000 | bytes 3200000 | tf_op jit(solution)/shard_map/grad/pallas_call | solution.py:124
  76.6 4.4 %fusion.9 = bf16[2,128,3584]{2,1,0:T(8,128)(2,1)S(1)} fusion(bf16[2,128,768]{2,1,0:T(8,128)(2,1)} %get-tuple-element.8, bf16[3584,768]{1,0:T(8,128)(2,1)} %param.4), kind=kOutput, calls=%fused_computation.10 | convolution fusion | flops 1410203648 | bytes 7733248 | tf_op jit(solution)/shard_map/dot_general | solution.py:164
  81.6 3.4 %collective-permute-done.5 = bf16[2,128,3584]{2,1,0:T(8,128)(2,1)S(1)} collective-permute-done((bf16[2,128,3584]{2,1,0:T(8,128)(2,1)S(1)}, bf16[2,128,3584]{2,1,0:T(8,128)(2,1)S(1)}, u32[]{:S(2)}, u32[]{:S(2)}) %collective-permute-start.5) | collective-permute-done | bytes 1835040 | tf_op jit(solution)/shard_map/ppermute | solution.py:46
  85.1 1.7 %add_convert_fusion = bf16[2,128,3584]{2,1,0:T(8,128)(2,1)S(1)} fusion(bf16[2,128,3584]{2,1,0:T(8,128)(2,1)S(1)} %collective-permute-done.5, bf16[2,128,768]{2,1,0:T(8,128)(2,1)S(1)} %copy-done.1, bf16[3584,768]{1,0:T(8,128)(2,1)S(1)} %bitcast.35), kind=kOutput, calls=%fused_computation.11 | convolution fusion | flops 1412038656 | bytes 9568256 | tf_op jit(solution)/shard_map/dot_general | solution.py:164
  87.6 12.7 %collective-permute-done.6 = bf16[2,64,3584]{2,1,0:T(8,128)(2,1)S(1)} collective-permute-done((bf16[2,64,3584]{2,1,0:T(8,128)(2,1)S(1)}, bf16[2,64,3584]{2,1,0:T(8,128)(2,1)S(1)}, u32[]{:S(2)}, u32[]{:S(2)}) %collective-permute-start.6) | collective-permute-done | bytes 917536 | tf_op jit(solution)/shard_map/ppermute | solution.py:42
  101.1 8.1 %collective-permute-done.7 = bf16[2,32,3584]{2,1,0:T(8,128)(2,1)} collective-permute-done((bf16[2,32,3584]{2,1,0:T(8,128)(2,1)S(1)}, bf16[2,32,3584]{2,1,0:T(8,128)(2,1)}, u32[]{:S(2)}, u32[]{:S(2)}) %collective-permute-start.7) | collective-permute-done | bytes 458784 | tf_op jit(solution)/shard_map/ppermute | solution.py:42
  109.2 1.1 add_convert_fusion.2
  111.3 1.6 %fusion.12 = f32[3584,768,1]{1,0,2:T(8,128)S(1)} fusion(bf16[2,128,3584]{2,1,0:T(8,128)(2,1)S(1)} %constant_dynamic-update-slice_fusion, bf16[2,128,768]{2,1,0:T(8,128)(2,1)S(1)} %copy-done.2), kind=kOutput, calls=%fused_computation.25 | convolution fusion | flops 1409286144 | bytes 13238272 | tf_op jit(solution)/shard_map/dot_general | solution.py:164
  113.0 9.3 %collective-permute-done.8 = bf16[2,16,3584]{2,1,0:T(8,128)(2,1)S(1)} collective-permute-done((bf16[2,16,3584]{2,1,0:T(8,128)(2,1)S(1)}, bf16[2,16,3584]{2,1,0:T(8,128)(2,1)S(1)}, u32[]{:S(2)}, u32[]{:S(2)}) %collective-permute-start.8) | collective-permute-done | bytes 229408 | tf_op jit(solution)/shard_map/ppermute | solution.py:42
  122.5 5.6 %fusion = bf16[3584,768]{1,0:T(8,128)(2,1)} fusion(f32[3584,768,1]{1,0,2:T(8,128)S(1)} %fusion.12, bf16[2,128,3584]{2,1,0:T(8,128)(2,1)} %collective-permute-done.4, bf16[2,128,768]{2,1,0:T(8,128)(2,1)S(1)} %copy-done), kind=kOutput, calls=%fused_computation.1 | convolution fusion | flops 1414791168 | bytes 18743296 | tf_op jit(solution)/shard_map/dot_general | solution.py:164
  (47 shorter events, 10.1 us)
Async XLA Ops:
  0.6 7.2 %collective-permute-start = (bf16[2,8,3584]{2,1,0:T(8,128)(2,1)}, bf16[2,8,3584]{2,1,0:T(8,128)(2,1)S(1)}, u32[]{:S(2)}, u32[]{:S(2)}) collective-permute-start(bf16[2,8,3584]{2,1,0:T(8,128)(2,1)} %param.3), channel_id=1, source_target_pairs={{0,8},{1,17},{2,10},{3,19},{4,12},{5,21},{6,14},{7,23},{8,0},{9,25... | collective-permute-start | bytes 344072 | tf_op jit(solution)/shard_map/ppermute | solution.py:42
  8.8 8.1 %collective-permute-start.1 = (bf16[2,16,3584]{2,1,0:T(8,128)(2,1)S(1)}, bf16[2,16,3584]{2,1,0:T(8,128)(2,1)S(1)}, u32[]{:S(2)}, u32[]{:S(2)}) collective-permute-start(bf16[2,16,3584]{2,1,0:T(8,128)(2,1)S(1)} %pad_maximum_fusion.2), channel_id=1, source_target_pairs={{0,16},{1,9},{2,18},{3,11},{4,20},{5,13},{6,22},{7,15},{8,24},{9,1... | collective-permute-start | bytes 688136 | tf_op jit(solution)/shard_map/ppermute | solution.py:42
  17.8 8.5 %collective-permute-start.2 = (bf16[2,32,3584]{2,1,0:T(8,128)(2,1)S(1)}, bf16[2,32,3584]{2,1,0:T(8,128)(2,1)S(1)}, u32[]{:S(2)}, u32[]{:S(2)}) collective-permute-start(bf16[2,32,3584]{2,1,0:T(8,128)(2,1)S(1)} %pad_maximum_fusion.1), channel_id=1, source_target_pairs={{0,2},{1,5},{2,0},{3,7},{4,6},{5,1},{6,4},{7,3},{8,10},{9,13},{10,... | collective-permute-start | bytes 1376264 | tf_op jit(solution)/shard_map/ppermute | solution.py:42
  27.3 13.5 %collective-permute-start.3 = (bf16[2,64,3584]{2,1,0:T(8,128)(2,1)S(1)}, bf16[2,64,3584]{2,1,0:T(8,128)(2,1)S(1)}, u32[]{:S(2)}, u32[]{:S(2)}) collective-permute-start(bf16[2,64,3584]{2,1,0:T(8,128)(2,1)S(1)} %pad_maximum_fusion), channel_id=1, source_target_pairs={{0,4},{1,3},{2,6},{3,1},{4,0},{5,7},{6,2},{7,5},{8,12},{9,11},{10,... | collective-permute-start | bytes 2752520 | tf_op jit(solution)/shard_map/ppermute | solution.py:42
  40.8 5.3 %slice-start = ((s8[5505024]{0:T(1024)(128)(4,1)}), s8[1310720]{0:T(1024)(128)(4,1)S(1)}, s32[]{:S(2)}) async-start(s8[5505024]{0:T(1024)(128)(4,1)} %bitcast.32), calls=%async_computation.1 | async-start | bytes 2621440
  40.8 5.3 %collective-permute-start.4 = (bf16[2,128,3584]{2,1,0:T(8,128)(2,1)S(1)}, bf16[2,128,3584]{2,1,0:T(8,128)(2,1)}, u32[]{:S(2)}, u32[]{:S(2)}) collective-permute-start(bf16[2,128,3584]{2,1,0:T(8,128)(2,1)S(1)} %constant_dynamic-update-slice_fusion), channel_id=1, source_target_pairs={{0,1},{1,0},{2,3},{3,2},{4,5},{5,4},{6,7},{7,6},{8,9},{9,8},{10,11... | collective-permute-start | bytes 5505032 | tf_op jit(solution)/shard_map/ppermute | solution.py:46
  40.9 5.2 %slice-start.1 = ((s8[5505024]{0:T(1024)(128)(4,1)}), s8[4194304]{0:T(1024)(128)(4,1)S(1)}, s32[]{:S(2)}) async-start(s8[5505024]{0:T(1024)(128)(4,1)} %bitcast.32), calls=%async_computation.2 | async-start | bytes 8388608
  73.5 11.5 %slice-start.2 = ((s8[5505024]{0:T(1024)(128)(4,1)}), s8[1310720]{0:T(1024)(128)(4,1)S(1)}, s32[]{:S(2)}) async-start(s8[5505024]{0:T(1024)(128)(4,1)} %bitcast.34), calls=%async_computation.3 | async-start | bytes 2621440
  76.6 8.4 %copy-start.1 = (bf16[2,128,768]{2,1,0:T(8,128)(2,1)S(1)}, bf16[2,128,768]{2,1,0:T(8,128)(2,1)}, u32[]{:S(2)}) copy-start(bf16[2,128,768]{2,1,0:T(8,128)(2,1)} %get-tuple-element.7) | copy-start | bytes 1179652
  76.6 8.4 %slice-start.3 = ((s8[5505024]{0:T(1024)(128)(4,1)}), s8[4194304]{0:T(1024)(128)(4,1)S(1)}, s32[]{:S(2)}) async-start(s8[5505024]{0:T(1024)(128)(4,1)} %bitcast.34), calls=%async_computation.4 | async-start | bytes 8388608
  81.1 4.0 %collective-permute-start.5 = (bf16[2,128,3584]{2,1,0:T(8,128)(2,1)S(1)}, bf16[2,128,3584]{2,1,0:T(8,128)(2,1)S(1)}, u32[]{:S(2)}, u32[]{:S(2)}) collective-permute-start(bf16[2,128,3584]{2,1,0:T(8,128)(2,1)S(1)} %fusion.9), channel_id=1, source_target_pairs={{0,1},{1,0},{2,3},{3,2},{4,5},{5,4},{6,7},{7,6},{8,9},{9,8},{10,11... | collective-permute-start | bytes 5505032 | tf_op jit(solution)/shard_map/ppermute | solution.py:46
  86.8 13.5 %collective-permute-start.6 = (bf16[2,64,3584]{2,1,0:T(8,128)(2,1)S(1)}, bf16[2,64,3584]{2,1,0:T(8,128)(2,1)S(1)}, u32[]{:S(2)}, u32[]{:S(2)}) collective-permute-start(bf16[2,64,3584]{2,1,0:T(8,128)(2,1)S(1)} %slice.33), channel_id=1, source_target_pairs={{0,4},{1,3},{2,6},{3,1},{4,0},{5,7},{6,2},{7,5},{8,12},{9,11},{10,... | collective-permute-start | bytes 2752520 | tf_op jit(solution)/shard_map/ppermute | solution.py:42
  100.6 8.6 %collective-permute-start.7 = (bf16[2,32,3584]{2,1,0:T(8,128)(2,1)S(1)}, bf16[2,32,3584]{2,1,0:T(8,128)(2,1)}, u32[]{:S(2)}, u32[]{:S(2)}) collective-permute-start(bf16[2,32,3584]{2,1,0:T(8,128)(2,1)S(1)} %slice.35), channel_id=1, source_target_pairs={{0,2},{1,5},{2,0},{3,7},{4,6},{5,1},{6,4},{7,3},{8,10},{9,13},{10,... | collective-permute-start | bytes 1376264 | tf_op jit(solution)/shard_map/ppermute | solution.py:42
  101.1 10.2 %copy-start.2 = (bf16[2,128,768]{2,1,0:T(8,128)(2,1)S(1)}, bf16[2,128,768]{2,1,0:T(8,128)(2,1)}, u32[]{:S(2)}) copy-start(bf16[2,128,768]{2,1,0:T(8,128)(2,1)} %get-tuple-element.7) | copy-start | bytes 1179652
  110.4 12.1 %copy-start = (bf16[2,128,768]{2,1,0:T(8,128)(2,1)S(1)}, bf16[2,128,768]{2,1,0:T(8,128)(2,1)}, u32[]{:S(2)}) copy-start(bf16[2,128,768]{2,1,0:T(8,128)(2,1)} %get-tuple-element.8) | copy-start | bytes 1179652
  110.4 11.9 %collective-permute-start.8 = (bf16[2,16,3584]{2,1,0:T(8,128)(2,1)S(1)}, bf16[2,16,3584]{2,1,0:T(8,128)(2,1)S(1)}, u32[]{:S(2)}, u32[]{:S(2)}) collective-permute-start(bf16[2,16,3584]{2,1,0:T(8,128)(2,1)S(1)} %slice.37), channel_id=1, source_target_pairs={{0,16},{1,9},{2,18},{3,11},{4,20},{5,13},{6,22},{7,15},{8,24},{9,1... | collective-permute-start | bytes 688136 | tf_op jit(solution)/shard_map/ppermute | solution.py:42
  122.4 5.7 %copy-start.3 = (f32[8,64]{1,0:T(8,128)S(1)}, f32[8,64]{1,0:T(8,128)}, u32[]{:S(2)}) copy-start(f32[8,64]{1,0:T(8,128)} %get-tuple-element.6) | copy-start | bytes 6148
  122.4 6.5 %collective-permute-start.9 = (bf16[2,8,3584]{2,1,0:T(8,128)(2,1)S(1)}, bf16[2,8,3584]{2,1,0:T(8,128)(2,1)S(1)}, u32[]{:S(2)}, u32[]{:S(2)}) collective-permute-start(bf16[2,8,3584]{2,1,0:T(8,128)(2,1)S(1)} %slice.39), channel_id=1, source_target_pairs={{0,8},{1,17},{2,10},{3,19},{4,12},{5,21},{6,14},{7,23},{8,0},{9,25... | collective-permute-start | bytes 344072 | tf_op jit(solution)/shard_map/ppermute | solution.py:42
